TPU v7x, 256 devices: a whole 4x4x8 slice. The times are simulated.
256 devices in a mesh: gx: 4 (over x), gy: 4 (over y), gz: 16 (over z, core).
Axes of the slice: x: 4, y: 4, z: 8, core: 2. Of those that a mesh axis runs over, the one named last changes fastest.
Arguments:
- densities: float32 [7, 512, 128, 512], P(None, 'gz', 'gy', 'gx'), may hold values from -6 to 6
- residuals: float32 [7, 512, 128, 512], P(None, 'gz', 'gy', 'gx'), may hold values from -320 to 320
Outputs:
- new_density: float32 [512, 128, 512], P('gz', 'gy', 'gx')
- weights: float32 [7], replicated
All inputs are finite; a program needn't handle non-finite values.
Results may differ from a plain program's by a relative error of at most 0.000087.
Values sent between devices are 32-bit elements; how exact they have to be, the bound alone decides.
A program may use at most 64 MiB of HBM per device.

v0:
```python
import math

import jax
import jax.numpy as jnp
from jax import lax
from jax.sharding import Mesh
from jax.sharding import PartitionSpec as P

SWEEPS = 3
GX_GY_GZ = ("gx", "gy", "gz_0", "gz_1")
GZ = ("gz_0", "gz_1")


shift_value = 0.15
mix_amount = 0.7


def extended(cells, sides, width):
    for axis, dim in sides:
        count = lax.axis_size(axis)
        head = lax.slice_in_dim(cells, 0, width, axis=dim)
        tail = lax.slice_in_dim(cells, cells.shape[dim] - width, cells.shape[dim], axis=dim)
        cells = jnp.concatenate(
            [
                lax.ppermute(tail, axis, [(i, (i + 1) % count) for i in range(count)]),
                cells,
                lax.ppermute(head, axis, [((i + 1) % count, i) for i in range(count)]),
            ],
            axis=dim,
        )
    return cells


def one_axis_at_a_time(shard, axes):
    for axis in axes:
        shard = lax.psum(shard, axis)
    return shard


def sweep_weights():
    diag_value = 6.0 + shift_value
    upper = (shift_value + 12.0) / diag_value
    lower = upper / 3.0
    return [
        1.0
        / (
            (upper + lower) / 2.0
            + (upper - lower) / 2.0 * math.cos(math.pi * (2 * k - 1) / (2 * SWEEPS))
        )
        for k in range(1, SWEEPS + 1)
    ]


def neighbours(padded):
    total = padded[:, 2:, 1:-1, 1:-1] + padded[:, :-2, 1:-1, 1:-1]
    total = total + padded[:, 1:-1, 2:, 1:-1] + padded[:, 1:-1, :-2, 1:-1]
    return total + padded[:, 1:-1, 1:-1, 2:] + padded[:, 1:-1, 1:-1, :-2]


def shrink(field):
    return field[:, 1:-1, 1:-1, 1:-1]


def relax(padded, rhs, omega):
    diag_value = 6.0 + shift_value
    centre = shrink(padded)
    return centre + omega * (rhs - diag_value * centre + neighbours(padded)) / diag_value


def precondition(fields):
    diag_value = 6.0 + shift_value
    omegas = sweep_weights()
    padded = extended(fields, (("gx", 3), ("gy", 2), (GZ, 1)), SWEEPS)
    rhs = 6.0 * shrink(padded) - neighbours(padded)
    iterate = omegas[0] * rhs / diag_value
    for position in range(1, SWEEPS):
        rhs = shrink(rhs)
        iterate = relax(iterate, rhs, omegas[position])
    return iterate


def on_device(densities, residuals):
    count = residuals.shape[0]
    flat = residuals.reshape(count, -1)
    local = jnp.dot(
        flat, flat.T, precision=lax.Precision.HIGHEST, preferred_element_type=jnp.float32
    )
    gram = one_axis_at_a_time(local, GX_GY_GZ)
    factor = jnp.linalg.cholesky(gram)
    ones_column = jnp.ones((count, 1), jnp.float32)
    middle = lax.linalg.triangular_solve(factor, ones_column, left_side=True, lower=True)
    solved = lax.linalg.triangular_solve(
        factor, middle, left_side=True, lower=True, transpose_a=True
    )[:, 0]
    weights = solved / jnp.sum(solved)
    blended = jnp.tensordot(weights, densities, axes=1, precision=lax.Precision.HIGHEST)
    combined = jnp.tensordot(weights, residuals, axes=1, precision=lax.Precision.HIGHEST)
    update = precondition(combined[None])[0]
    return (blended + mix_amount * update, weights)


def solution(mesh):
    torus = Mesh(
        mesh.devices.reshape(mesh.shape["gx"], mesh.shape["gy"], 8, 2), ("gx", "gy", "gz_0", "gz_1")
    )
    return jax.shard_map(
        on_device,
        mesh=torus,
        in_specs=(P(None, GZ, "gy", "gx"), P(None, GZ, "gy", "gx")),
        out_specs=(P(GZ, "gy", "gx"), P()),
        check_vma=False,
    )
```

profile of v0, /device:TPU:1, one launch (start us, length us, event | category | flops | bytes accessed | tf_op | source)
XLA Modules:
  0.0 107.2 jit_solution(10908965110666886729)
XLA Ops:
  0.6 14.5 %fusion.10 = f32[7,7]{0,1:T(8,128)S(1)} fusion(f32[7,32,32,128]{3,2,1,0:T(8,128)} %param.3), kind=kOutput, calls=%fused_computation.23 | convolution fusion | flops 77070336 | bytes 3670212 | tf_op jit(solution)/shard_map/dot_general | solution.py:85
  15.1 9.3 %psum.28 = f32[7,7]{0,1:T(8,128)S(1)} all-reduce(f32[7,7]{0,1:T(8,128)S(1)} %fusion.10), channel_id=1, replica_groups=mesh['gx'=4,'gy'=4,'gz_0'=8,'gz_1'=2] {'gx'}, use_global_device_ids=true, to_apply=%region_0.0 | all-reduce | flops 49 | bytes 392 | tf_op jit(solution)/shard_map/psum | solution.py:36
  24.4 9.0 %psum.29 = f32[7,7]{0,1:T(8,128)S(1)} all-reduce(f32[7,7]{0,1:T(8,128)S(1)} %psum.28), channel_id=1, replica_groups=mesh['gx'=4,'gy'=4,'gz_0'=8,'gz_1'=2] {'gy'}, use_global_device_ids=true, to_apply=%region_1.0 | all-reduce | flops 49 | bytes 392 | tf_op jit(solution)/shard_map/psum | solution.py:36
  33.4 16.2 %psum.30 = f32[7,7]{0,1:T(8,128)S(1)} all-reduce(f32[7,7]{0,1:T(8,128)S(1)} %psum.29), channel_id=1, replica_groups=mesh['gx'=4,'gy'=4,'gz_0'=8,'gz_1'=2] {'gz_0'}, use_global_device_ids=true, to_apply=%region_2.0 | all-reduce | flops 49 | bytes 392 | tf_op jit(solution)/shard_map/psum | solution.py:36
  49.6 10.4 %psum.31 = f32[7,7]{0,1:T(8,128)S(1)} all-reduce(f32[7,7]{0,1:T(8,128)S(1)} %psum.30), channel_id=1, replica_groups=mesh['gx'=4,'gy'=4,'gz_0'=8,'gz_1'=2] {'gz_1'}, use_global_device_ids=true, to_apply=%region_3.0 | all-reduce | flops 49 | bytes 392 | tf_op jit(solution)/shard_map/psum | solution.py:36
  59.9 0.1 copy.7
  60.1 0.6 cholesky.16
  60.7 0.6 compare_reduce_fusion
  61.4 0.6 fusion.19
  62.0 0.5 custom-call.8
  62.6 0.1 convolution_bitcast_fusion.1
  62.7 0.8 fusion.29
  63.4 0.6 broadcast_divide_fusion
  64.1 0.0 copy-start.1
  64.1 7.8 %fusion = f32[1,32,32,128]{3,0,2,1:T(1,128)S(1)} fusion(f32[7,32,32,128]{3,2,1,0:T(8,128)} %param.3, f32[7]{0:T(128)S(1)} %broadcast_divide_fusion), kind=kOutput, calls=%fused_computation | convolution fusion | flops 11010048 | bytes 4194332 | tf_op jit(solution)/shard_map/dot_general | solution.py:97
  72.0 0.2 fusion.28
  72.2 0.1 collective-permute-start
  72.3 2.7 %collective-permute-start.1 = (f32[1,32,32,3]{3,2,1,0:T(8,128)S(1)}, f32[1,32,32,3]{3,2,1,0:T(8,128)S(1)}, u32[]{:S(2)}, u32[]{:S(2)}) collective-permute-start(f32[1,32,32,3]{3,2,1,0:T(8,128)S(1)} %get-tuple-element.9), channel_id=1, source_target_pairs={{64,0},{128,64},{192,128},{0,192},{65,1},{129,65},{193,129},{1,193... | collective-permute-start | bytes 36872 | tf_op jit(solution)/shard_map/ppermute | solution.py:27
  74.9 11.7 %collective-permute-done = f32[1,32,32,3]{3,2,1,0:T(8,128)S(1)} collective-permute-done((f32[1,32,32,3]{3,2,1,0:T(8,128)S(1)}, f32[1,32,32,3]{3,2,1,0:T(8,128)S(1)}, u32[]{:S(2)}, u32[]{:S(2)}) %collective-permute-start) | collective-permute-done | bytes 12320 | tf_op jit(solution)/shard_map/ppermute | solution.py:25
  86.6 0.0 collective-permute-done.1
  86.6 0.3 pad_maximum_fusion.3
  86.9 0.1 collective-permute-start.2
  87.0 2.7 %collective-permute-start.3 = (f32[1,32,3,134]{3,2,1,0:T(4,128)S(1)}, f32[1,32,3,134]{3,2,1,0:T(4,128)S(1)}, u32[]{:S(2)}, u32[]{:S(2)}) collective-permute-start(f32[1,32,3,134]{3,2,1,0:T(4,128)S(1)} %get-tuple-element.7), channel_id=1, source_target_pairs={{16,0},{32,16},{48,32},{0,48},{17,1},{33,17},{49,33},{1,49},{18,2}... | collective-permute-start | bytes 154376 | tf_op jit(solution)/shard_map/ppermute | solution.py:27
  89.6 2.4 %collective-permute-done.2 = f32[1,32,3,134]{3,2,1,0:T(4,128)S(1)} collective-permute-done((f32[1,32,3,134]{3,2,1,0:T(4,128)S(1)}, f32[1,32,3,134]{3,2,1,0:T(4,128)S(1)}, u32[]{:S(2)}, u32[]{:S(2)}) %collective-permute-start.2) | collective-permute-done | bytes 51488 | tf_op jit(solution)/shard_map/ppermute | solution.py:25
  92.0 0.2 pad_maximum_fusion.8
  92.2 1.8 %collective-permute-start.4 = (f32[1,3,38,134]{3,2,1,0:T(8,128)S(1)}, f32[1,3,38,134]{3,2,1,0:T(8,128)S(1)}, u32[]{:S(2)}, u32[]{:S(2)}) collective-permute-start(f32[1,3,38,134]{3,2,1,0:T(8,128)S(1)} %get-tuple-element.4), channel_id=1, source_target_pairs={{0,1},{1,2},{2,3},{3,4},{4,5},{5,6},{6,7},{7,8},{8,9},{9,10},{10,1... | collective-permute-start | bytes 183320 | tf_op jit(solution)/shard_map/ppermute | solution.py:25
  93.9 0.6 collective-permute-start.5
  94.6 5.2 %fusion.4 = f32[1,32,32,128]{3,0,2,1:T(1,128)S(1)} fusion(f32[7,32,32,128]{3,2,1,0:T(8,128)S(1)} %copy-done, f32[7]{0:T(128)S(1)} %broadcast_divide_fusion), kind=kOutput, calls=%fused_computation.4 | convolution fusion | flops 11010048 | bytes 4194332 | tf_op jit(solution)/shard_map/dot_general | solution.py:96
  99.8 0.6 pad_maximum_fusion
  100.4 2.3 %broadcast_multiply_fusion = (f32[1,36,36,132]{3,2,1,0:T(8,128)S(1)}, f32[1,36,36,132]{3,2,1,0:T(8,128)S(1)}) fusion(f32[1,38,38,134]{3,2,1,0:T(8,128)S(1)} %pad_maximum_fusion), kind=kLoop, calls=%fused_computation.26 | loop fusion | flops 1368576 | bytes 6158592 | tf_op jit(solution)/shard_map/div | solution.py:75
  102.7 2.6 %fusion.9 = f32[1,34,34,130]{3,2,1,0:T(8,128)S(1)} fusion(f32[1,36,36,132]{3,2,1,0:T(8,128)S(1)} %get-tuple-element.2, f32[1,36,36,132]{3,2,1,0:T(8,128)S(1)} %get-tuple-element.3), kind=kLoop, calls=%fused_computation.17 | loop fusion | flops 1502800 | bytes 5410080 | tf_op jit(solution)/shard_map/add | solution.py:67
  105.3 1.8 %fusion.18 = f32[32,32,128]{2,1,0:T(8,128)} fusion(f32[32,32,128]{2,1,0:T(8,128)S(1)} %bitcast.45, f32[1,34,34,130]{3,2,1,0:T(8,128)S(1)} %fusion.9, f32[1,36,36,132]{3,2,1,0:T(8,128)S(1)} %get-tuple-element.3), kind=kLoop, calls=%fused_computation.33 | loop fusion | flops 1572864 | bytes 5242880 | tf_op jit(solution)/shard_map/add | solution.py:99
  (8 shorter events, 0.1 us)
Async XLA Ops:
  64.1 30.5 %copy-start.1 = (f32[7]{0:T(128)}, f32[7]{0:T(128)S(1)}, u32[]{:S(2)}) copy-start(f32[7]{0:T(128)S(1)} %broadcast_divide_fusion) | copy-start | bytes 88
  72.2 14.4 %collective-permute-start = (f32[1,32,32,3]{3,2,1,0:T(8,128)S(1)}, f32[1,32,32,3]{3,2,1,0:T(8,128)S(1)}, u32[]{:S(2)}, u32[]{:S(2)}) collective-permute-start(f32[1,32,32,3]{3,2,1,0:T(8,128)S(1)} %get-tuple-element.8), channel_id=1, source_target_pairs={{0,64},{64,128},{128,192},{192,0},{1,65},{65,129},{129,193},{193,1... | collective-permute-start | bytes 36872 | tf_op jit(solution)/shard_map/ppermute | solution.py:25
  72.3 14.3 %collective-permute-start.1 = (f32[1,32,32,3]{3,2,1,0:T(8,128)S(1)}, f32[1,32,32,3]{3,2,1,0:T(8,128)S(1)}, u32[]{:S(2)}, u32[]{:S(2)}) collective-permute-start(f32[1,32,32,3]{3,2,1,0:T(8,128)S(1)} %get-tuple-element.9), channel_id=1, source_target_pairs={{64,0},{128,64},{192,128},{0,192},{65,1},{129,65},{193,129},{1,193... | collective-permute-start | bytes 36872 | tf_op jit(solution)/shard_map/ppermute | solution.py:27
  86.6 8.0 %copy-start = (f32[7,32,32,128]{3,2,1,0:T(8,128)S(1)}, f32[7,32,32,128]{3,2,1,0:T(8,128)}, u32[]{:S(2)}) copy-start(f32[7,32,32,128]{3,2,1,0:T(8,128)} %param.2) | copy-start | bytes 11010052
  86.9 5.1 %collective-permute-start.2 = (f32[1,32,3,134]{3,2,1,0:T(4,128)S(1)}, f32[1,32,3,134]{3,2,1,0:T(4,128)S(1)}, u32[]{:S(2)}, u32[]{:S(2)}) collective-permute-start(f32[1,32,3,134]{3,2,1,0:T(4,128)S(1)} %get-tuple-element.6), channel_id=1, source_target_pairs={{0,16},{16,32},{32,48},{48,0},{1,17},{17,33},{33,49},{49,1},{2,18}... | collective-permute-start | bytes 154376 | tf_op jit(solution)/shard_map/ppermute | solution.py:25
  87.0 5.0 %collective-permute-start.3 = (f32[1,32,3,134]{3,2,1,0:T(4,128)S(1)}, f32[1,32,3,134]{3,2,1,0:T(4,128)S(1)}, u32[]{:S(2)}, u32[]{:S(2)}) collective-permute-start(f32[1,32,3,134]{3,2,1,0:T(4,128)S(1)} %get-tuple-element.7), channel_id=1, source_target_pairs={{16,0},{32,16},{48,32},{0,48},{17,1},{33,17},{49,33},{1,49},{18,2}... | collective-permute-start | bytes 154376 | tf_op jit(solution)/shard_map/ppermute | solution.py:27
  92.2 7.6 %collective-permute-start.4 = (f32[1,3,38,134]{3,2,1,0:T(8,128)S(1)}, f32[1,3,38,134]{3,2,1,0:T(8,128)S(1)}, u32[]{:S(2)}, u32[]{:S(2)}) collective-permute-start(f32[1,3,38,134]{3,2,1,0:T(8,128)S(1)} %get-tuple-element.4), channel_id=1, source_target_pairs={{0,1},{1,2},{2,3},{3,4},{4,5},{5,6},{6,7},{7,8},{8,9},{9,10},{10,1... | collective-permute-start | bytes 183320 | tf_op jit(solution)/shard_map/ppermute | solution.py:25
  93.9 5.8 %collective-permute-start.5 = (f32[1,3,38,134]{3,2,1,0:T(8,128)S(1)}, f32[1,3,38,134]{3,2,1,0:T(8,128)S(1)}, u32[]{:S(2)}, u32[]{:S(2)}) collective-permute-start(f32[1,3,38,134]{3,2,1,0:T(8,128)S(1)} %get-tuple-element.5), channel_id=1, source_target_pairs={{1,0},{2,1},{3,2},{4,3},{5,4},{6,5},{7,6},{8,7},{9,8},{10,9},{11,1... | collective-permute-start | bytes 183320 | tf_op jit(solution)/shard_map/ppermute | solution.py:27
where the time goes:
time: 109 us; the launch traced here: 107 us
  blocking collectives  44.8 us (41%)
  matrix products  28.4 us (26%)
  waiting for transfers between devices  14 us (13%)
  other arithmetic  11 us (10%)
  starting transfers between devices  7.88 us (7%)
    psum x4, blocking collectives, one_axis_at_a_time(): shard = lax.psum(shard, axis)  44.8 us
    dot_general x1, matrix products, on_device(): jnp.dot(flat, flat.T, precision=lax.Precision.HIGHEST, preferred_element_...  14.5 us
    ppermute x3, waiting for transfers between devices, extended(): lax.ppermute(tail, axis, [(i, (i + 1) % count) for i in range(count)])  14 us
    dot_general x1, matrix products, on_device(): jnp.tensordot(weights, residuals, axes=1, precision=lax.Precision.HIGHEST)  7.85 us
    ppermute x3, starting transfers between devices, extended(): lax.ppermute(head, axis, [((i + 1) % count, i) for i in range(count)])  5.95 us
    dot_general x1, matrix products, on_device(): jnp.tensordot(weights, densities, axes=1, precision=lax.Precision.HIGHEST)  5.18 us
    add x1, other arithmetic, relax(): centre + omega * (rhs - diag_value * centre + neighbours(padded)) / diag_...  2.59 us
    div x1, other arithmetic, precondition(): iterate = omegas[0] * rhs / diag_value  2.35 us
  transfers between devices with their start and end apart: 6, of which 2 were waited for; matrix products, arithmetic and copies ran while one was open for 5% of the time, Pallas kernels for 0%

commit v1 on v0

v1 whole, which is shorter than its diff:
```python
import functools
import itertools
import math

import jax
import jax.numpy as jnp
from jax import lax
from jax.experimental import pallas as pl
from jax.experimental.pallas import tpu as pltpu
from jax.sharding import PartitionSpec as P

MESH = pl.DeviceIdType.MESH
HIST = 7
SWEEPS = 3
HALO = 3
SHIFT = 0.15
MIX = 0.7
DIAG = 6.0 + SHIFT
PAIRS = [(i, j) for i in range(HIST) for j in range(i + 1)]
ZR = 5
SLOT = 16


def sweep_weights():
    upper = (SHIFT + 12.0) / DIAG
    lower = upper / 3.0
    return [
        1.0
        / (
            (upper + lower) / 2.0
            + (upper - lower) / 2.0 * math.cos(math.pi * (2 * k - 1) / (2 * SWEEPS))
        )
        for k in range(1, SWEEPS + 1)
    ]


W1, W2, W3 = sweep_weights()
A2 = ((1.0 - W2) * W1 + W2) / DIAG
B2 = W2 * W1 / DIAG / DIAG
K1 = MIX * (1.0 - W3)
K2 = MIX * W3 / DIAG


def lanes(shape):
    return lax.broadcasted_iota(jnp.int32, shape, len(shape) - 1)


def pulay(total):
    gram = {}
    for k, (i, j) in enumerate(PAIRS):
        gram[i, j] = jnp.broadcast_to(total[:, k : k + 1], (8, 128))
    low, inv, mid = {}, [], []
    for j in range(HIST):
        pivot = gram[j, j]
        for k in range(j):
            pivot = pivot - low[j, k] * low[j, k]
        inv.append(lax.rsqrt(pivot))
        for i in range(j + 1, HIST):
            value = gram[i, j]
            for k in range(j):
                value = value - low[i, k] * low[j, k]
            low[i, j] = value * inv[j]
        value = 1.0
        for k in range(j):
            value = value - low[j, k] * mid[k]
        mid.append(value * inv[j])
    solved = [None] * HIST
    for j in reversed(range(HIST)):
        value = mid[j]
        for k in range(j + 1, HIST):
            value = value - low[k, j] * solved[k]
        solved[j] = value * inv[j]
    scale = 1.0 / functools.reduce(jnp.add, solved)
    return [value * scale for value in solved]


def exchange(sizes, dens, res, acc, from_left, from_right, own_left, own_right, weights,
             R, D, C, T1, T2, G1, G2, load_sem, dens_sem, bulk_send, bulk_recv,
             edge_send, edge_recv, gram_send, gram_recv):
    NX, NY, NZ = sizes
    nz, ny = res.shape[1], res.shape[2]
    ring = R.shape[2]
    gx, gy, gz = lax.axis_index("gx"), lax.axis_index("gy"), lax.axis_index("gz")

    def device(dx=0, dy=0, dz=0):
        return {
            "gx": lax.rem(gx + dx % NX, NX),
            "gy": lax.rem(gy + dy % NY, NY),
            "gz": lax.rem(gz + dz % NZ, NZ),
        }

    plane_peers = [device(dx=a, dy=b) for a, b in itertools.product(range(NX), range(NY)) if a or b]
    line_peers = [device(dz=c) for c in range(1, NZ)]
    corner_peers = [device(dy=b, dz=c) for b in (-1, 1) for c in (-1, 1)]
    barrier = pltpu.get_barrier_semaphore()
    greeted = plane_peers + line_peers + corner_peers
    for peer in greeted:
        pl.semaphore_signal(barrier, inc=1, device_id=peer, device_id_type=MESH)

    chunks = load_sem.shape[0]
    depth = nz // chunks
    loads = []
    for c in range(chunks):
        copy = pltpu.make_async_copy(
            res.at[:, pl.ds(c * depth, depth)],
            R.at[:, pl.ds(HALO + c * depth, depth), pl.ds(0, ny)],
            load_sem.at[c],
        )
        copy.start()
        loads.append(copy)
    dens_copy = pltpu.make_async_copy(dens, D, dens_sem)
    dens_copy.start()

    def plane_products(z, sums):
        sums = list(sums)
        for t in range(ny // 8):
            rows = [R[i, HALO + z, 8 * t : 8 * t + 8, :] for i in range(HIST)]
            for k, (i, j) in enumerate(PAIRS):
                sums[k] = sums[k] + rows[i] * rows[j]
        return tuple(sums)

    sums = tuple(jnp.zeros((8, 128), jnp.float32) for _ in PAIRS)
    for c in range(chunks):
        loads[c].wait()
        sums = lax.fori_loop(c * depth, (c + 1) * depth, plane_products, sums)
    lane = lanes((8, 128))
    partial = jnp.zeros((8, 128), jnp.float32)
    for k in range(len(PAIRS)):
        partial = jnp.where(lane == k, jnp.sum(sums[k], axis=1, keepdims=True), partial)
    row = jnp.sum(partial, axis=0, keepdims=True)

    pl.semaphore_wait(barrier, len(greeted))

    def share(buf, slot, value, peers, phase):
        buf[slot] = value
        for peer in peers:
            pltpu.make_async_remote_copy(
                buf.at[slot], buf.at[slot], gram_send.at[phase], gram_recv.at[phase],
                device_id=peer, device_id_type=MESH,
            ).start()
        return buf.at[pl.ds(0, len(peers))]

    def summed(buf, others, phase):
        pltpu.make_async_copy(others, others, gram_recv.at[phase]).wait()
        total = buf[0]
        for k in range(1, buf.shape[0]):
            total = total + buf[k]
        return total

    others1 = share(G1, gx * NY + gy, row, plane_peers, 0)

    main = pl.ds(HALO, nz)
    inner = pl.ds(0, ny)
    end_z = HALO + nz
    moves = [
        (res.at[:, pl.ds(0, 3)], R.at[:, pl.ds(end_z, 3), inner], device(dz=-1)),
        (res.at[:, pl.ds(nz - 3, 3)], R.at[:, pl.ds(0, 3), inner], device(dz=1)),
    ]
    for sy, sz in itertools.product((-1, 1), (-1, 1)):
        zs, zd = (0, end_z) if sz < 0 else (nz - 2, 1)
        ys, yd = (0, ny) if sy < 0 else (ny - 2, ring - 2)
        moves.append((
            res.at[:, pl.ds(zs, 2), pl.ds(ys, 2)],
            R.at[:, pl.ds(zd, 2), pl.ds(yd, 2)],
            device(dy=sy, dz=sz),
        ))
    moves += [
        (res.at[:, :, pl.ds(0, 3)], R.at[:, main, pl.ds(ny, 3)], device(dy=-1)),
        (res.at[:, :, pl.ds(ny - 3, 3)], R.at[:, main, pl.ds(ring - 3, 3)], device(dy=1)),
    ]
    bulk = [
        pltpu.make_async_remote_copy(
            src, dst, bulk_send.at[k], bulk_recv.at[k], device_id=peer, device_id_type=MESH
        )
        for k, (src, dst, peer) in enumerate(moves)
    ]
    for copy in bulk:
        copy.start()

    others2 = share(G2, gz, summed(G1, others1, 0), line_peers, 1)
    total = summed(G2, others2, 1)
    shares = pulay(total)
    for i in range(HIST):
        weights[i] = shares[i]
    shares = [weights[i] for i in range(HIST)]
    for copy in bulk:
        copy.wait_recv()

    tiles = ring // 8

    def combine(k):
        out = None
        for i in range(HIST):
            term = shares[i][None] * R[i, k].reshape(tiles, 8, 128)
            out = term if out is None else out + term
        return out.reshape(ring, 128)

    for k in (0, nz + 2 * HALO - 1):
        C[k] = combine(k)
    wide = lanes((ring, 128))

    def combine_pack(p, packs):
        value = combine(p + 1)
        C[p + 1] = value
        base = (p // ZR) * SLOT + lax.rem(p, ZR) * HALO
        here = (wide >= base) & (wide < base + HALO)
        left, right = packs
        left = jnp.where(here, pltpu.roll(value, base, 1), left)
        right = jnp.where(here, pltpu.roll(value, base + HALO, 1), right)
        return left, right

    empty = jnp.zeros((ring, 128), jnp.float32)
    left, right = lax.fori_loop(0, nz + 4, combine_pack, (empty, empty))
    own_left[...] = left
    own_right[...] = right
    edges = [
        pltpu.make_async_remote_copy(
            own_left, from_right, edge_send.at[0], edge_recv.at[0],
            device_id=device(dx=-1), device_id_type=MESH,
        ),
        pltpu.make_async_remote_copy(
            own_right, from_left, edge_send.at[1], edge_recv.at[1],
            device_id=device(dx=1), device_id_type=MESH,
        ),
    ]
    for copy in edges:
        copy.start()

    first, last = wide == 0, wide == 127

    def around(v):
        total = pltpu.roll(v, 1, 0) + pltpu.roll(v, ring - 1, 0)
        total = total + jnp.where(first, 0.0, pltpu.roll(v, 1, 1))
        return total + jnp.where(last, 0.0, pltpu.roll(v, 127, 1))

    def sweep1(k, _):
        v = C[k + 1]
        T1[k] = 6.0 * v - (C[k] + C[k + 2] + around(v))
        return 0

    def sweep2(k, _):
        v = T1[k + 1]
        T2[k] = A2 * v + B2 * (T1[k] + T1[k + 2] + around(v))
        return 0

    def sweep3(k, _):
        v = T2[k + 1]
        out = K1 * v + K2 * (T1[k + 2] + T2[k] + T2[k + 2] + around(v))
        out = out[:ny].reshape(ny // 8, 8, 128)
        for i in range(HIST):
            out = out + shares[i][None] * D[i, k].reshape(ny // 8, 8, 128)
        acc[k] = out.reshape(ny, 128)
        return 0

    lax.fori_loop(0, nz + 4, sweep1, 0)
    lax.fori_loop(0, nz + 2, sweep2, 0)
    dens_copy.wait()
    lax.fori_loop(0, nz, sweep3, 0)

    for copy in edges:
        copy.wait()
    for copy in bulk:
        copy.wait_send()
    for phase, others in enumerate((others1, others2)):
        pltpu.make_async_copy(others, others, gram_send.at[phase]).wait()


def finish(acc, from_left, from_right, own_left, own_right, weights, out, coeffs, buf, sem):
    nz, ny = acc.shape[0], acc.shape[1]
    ring = from_left.shape[0]
    wide = lanes((ring, 128))
    place = wide % SLOT
    inside = (place >= HALO) & (place < 3 * HALO)

    packs = (from_left[...], own_left[...], own_right[...], from_right[...])

    def spread(zr):
        value = jnp.zeros((ring, 128), jnp.float32)
        for q, pack in enumerate(packs):
            moved = pltpu.roll(pack, (HALO * (q - zr)) % 128, 1)
            value = jnp.where((place >= HALO * q) & (place < HALO * (q + 1)), moved, value)
        return value

    def nb(v):
        out = []
        for zr in range(ZR):
            before = v[zr - 1] if zr else pltpu.roll(v[ZR - 1], SLOT, 1)
            after = v[zr + 1] if zr < ZR - 1 else pltpu.roll(v[0], 128 - SLOT, 1)
            total = before + after
            total = total + pltpu.roll(v[zr], 1, 0) + pltpu.roll(v[zr], ring - 1, 0)
            out.append(total + pltpu.roll(v[zr], 1, 1) + pltpu.roll(v[zr], 127, 1))
        return out

    def relaxed(start, keep):
        n0 = nb(start)
        r = [keep(6.0 * v - n) for v, n in zip(start, n0)]
        n1 = nb(r)
        u = [keep(A2 * v + B2 * n) for v, n in zip(r, n1)]
        n2 = nb(u)
        return [K1 * v + K2 * (s + n) for v, s, n in zip(u, r, n2)]

    def clip(v):
        return jnp.where(inside, v, 0.0)

    whole = [spread(zr) for zr in range(ZR)]
    true = relaxed(whole, lambda v: v)
    closed = relaxed([clip(v) for v in whole], clip)
    change = [(a - b)[:ny] for a, b in zip(true, closed)]
    lane = lanes((ny, 128))
    near, far = lane < HALO, lane >= 128 - HALO
    chunks = sem.shape[0]
    copies = []
    for z in range(nz):
        zq, zr = divmod(z + 2, ZR)
        at_left = pltpu.roll(change[zr], (-(SLOT * zq + HALO)) % 128, 1)
        at_right = pltpu.roll(change[zr], (125 - (SLOT * zq + 2 * HALO)) % 128, 1)
        buf[z] = acc[z] + jnp.where(near, at_left, jnp.where(far, at_right, 0.0))
        depth = nz // chunks
        if z % depth == depth - 1:
            c = z // depth
            part = pl.ds(c * depth, depth)
            copy = pltpu.make_async_copy(buf.at[part], out.at[part], sem.at[c])
            copy.start()
            copies.append(copy)
    coeff_lane = lanes((1, 128))
    row = jnp.zeros((1, 128), jnp.float32)
    for i in range(HIST):
        row = jnp.where(coeff_lane == i, weights[i, 0:1, :], row)
    coeffs[...] = row[:, :HIST]
    for copy in copies:
        copy.wait()


def on_device(sizes, densities, residuals):
    _, nz, ny, nx = residuals.shape
    ring, deep = ny + 8, nz + 2 * HALO
    f32 = jnp.float32
    vmem, hbm = pl.BlockSpec(memory_space=pltpu.VMEM), pl.BlockSpec(memory_space=pltpu.HBM)
    edge = pltpu.VMEM((ring, nx), f32)
    NX, NY, NZ = sizes
    dma = pltpu.SemaphoreType.DMA
    middle = pl.pallas_call(
        functools.partial(exchange, sizes),
        out_shape=(
            pltpu.VMEM((nz, ny, nx), f32), edge, edge, edge, edge,
            pltpu.VMEM((HIST, 8, 128), f32),
        ),
        in_specs=[hbm, hbm],
        out_specs=(vmem,) * 6,
        scratch_shapes=[
            pltpu.VMEM((HIST, deep, ring, nx), f32),
            pltpu.VMEM((HIST, nz, ny, nx), f32),
            pltpu.VMEM((deep, ring, nx), f32),
            pltpu.VMEM((deep - 2, ring, nx), f32),
            pltpu.VMEM((deep - 4, ring, nx), f32),
            pltpu.VMEM((NX * NY, 1, 128), f32),
            pltpu.VMEM((NZ, 1, 128), f32),
            dma((8,)), dma(()), dma((8,)), dma((8,)), dma((2,)), dma((2,)), dma((2,)), dma((2,)),
        ],
        compiler_params=pltpu.CompilerParams(
            collective_id=0, has_side_effects=True, vmem_limit_bytes=60 << 20
        ),
    )(densities, residuals)
    density, coeffs = pl.pallas_call(
        finish,
        out_shape=(
            jax.ShapeDtypeStruct((nz, ny, nx), f32),
            jax.ShapeDtypeStruct((1, HIST), f32),
        ),
        in_specs=[vmem] * 6,
        out_specs=(hbm, vmem),
        scratch_shapes=[pltpu.VMEM((nz, ny, nx), f32), dma((4,))],
        compiler_params=pltpu.CompilerParams(vmem_limit_bytes=16 << 20),
    )(*middle)
    return density, coeffs.reshape(HIST)


def solution(mesh):
    sizes = tuple(mesh.shape[a] for a in ("gx", "gy", "gz"))
    spec = P(None, "gz", "gy", "gx")
    return jax.shard_map(
        functools.partial(on_device, sizes),
        mesh=mesh,
        in_specs=(spec, spec),
        out_specs=(P("gz", "gy", "gx"), P()),
        check_vma=False,
    )
```

time: 109 us -> 35.4 us (0.32); the launches traced: 107 us -> 35.4 us
  blocking collectives: 44.8 us -> 0 us
  Pallas kernels: 0 us -> 34.7 us
  matrix products: 28.4 us -> 0 us
  waiting for transfers between devices: 14 us -> 0 us
  other arithmetic: 11 us -> 0 us
  starting transfers between devices: 7.88 us -> 0 us
    psum x4 -> x0, blocking collectives: 44.8 us -> none  [one_axis_at_a_time(): shard = lax.psum(shard, axis)]
    pallas_call x0 -> x2, Pallas kernels: none -> 34.7 us  [the longest x1 32.4 us: on_device(): pl.pallas_call(functools.partial(exchange, sizes), out_shape=(pltpu.VMEM(...]
    dot_general x3 -> x0, matrix products: 27.5 us -> none  [the longest x1 14.5 us: on_device(): jnp.dot(flat, flat.T, precision=lax.Precision.HIGHEST, preferred_element_...]
    ppermute x6 -> x0, waiting for transfers between devices: 14 us -> none  [the longest x3 14 us: extended(): lax.ppermute(tail, axis, [(i, (i + 1) % count) for i in range(count)])]
    ppermute x6 -> x0, starting transfers between devices: 7.88 us -> none  [the longest x3 5.95 us: extended(): lax.ppermute(head, axis, [((i + 1) % count, i) for i in range(count)])]
    add x2 -> x0, other arithmetic: 4.43 us -> none  [the longest x1 2.59 us: relax(): centre + omega * (rhs - diag_value * centre + neighbours(padded)) / diag_...]
    div x3 -> x0, other arithmetic: 3 us -> none  [the longest x1 2.35 us: precondition(): iterate = omegas[0] * rhs / diag_value]
    another operation x5 -> x0, other arithmetic: 2.5 us -> none  [the longest x3 1.3 us: on_device(): factor = jnp.linalg.cholesky(gram)]
  transfers between devices with their start and end apart: 6 -> 0, of which waited for: 2 -> 0; matrix products, arithmetic and copies ran while one was open for 5% -> 0% of each run, Pallas kernels for 0% -> 0%
where the time goes in v1:
time: 35.4 us
  Pallas kernels  34.7 us (98%)
  between operations  0.64 us (2%)
    pallas_call x1, Pallas kernels, on_device(): pl.pallas_call(functools.partial(exchange, sizes), out_shape=(pltpu.VMEM(...  32.4 us
    pallas_call x1, Pallas kernels, on_device(): pl.pallas_call(finish, out_shape=(jax.ShapeDtypeStruct((nz, ny, nx), f32)...  2.35 us

profile of v1, /device:TPU:1, one launch (start us, length us, event | category | flops | bytes accessed | tf_op | source)
XLA Modules:
  0.0 35.4 jit_solution(2030798814564871352)
XLA Ops:
  0.6 32.4 %shard_map.41 = (f32[32,32,128]{2,1,0:T(8,128)S(1)}, f32[40,128]{1,0:T(8,128)S(1)}, f32[40,128]{1,0:T(8,128)S(1)}, f32[40,128]{1,0:T(8,128)S(1)}, f32[40,128]{1,0:T(8,128)S(1)}, /*index=5*/f32[7,8,128]{2,1,0:T(8,128)S(1)}) custom-call(f32[7,32,32,128]{3,2,1,0:T(8,128)} %dens.1, f32[7,32,32,128]{3,2,1,0:T(8,128)} %res.1), custom_call_target="tpu_custom_call" | custom-call | tf_op jit(solution)/shard_map/pallas_call | solution.py:342
  33.0 2.3 %shard_map.42 = (f32[32,32,128]{2,1,0:T(8,128)}, f32[1,7]{1,0:T(1,128)}) custom-call(f32[32,32,128]{2,1,0:T(8,128)S(1)} %get-tuple-element.10.acc, f32[40,128]{1,0:T(8,128)S(1)} %get-tuple-element.11.from_left, f32[40,128]{1,0:T(8,128)S(1)} %get-tuple-element.12.from_right, f32[40,128]{1,0:T(8,128)S(1)} %get-tuple-element.13.own_left, ...), custom_call_target="tpu_custom_call" | custom-call | tf_op jit(solution)/shard_map/pallas_call | solution.py:364

commit v2 on v1

v2 whole, which is shorter than its diff:
```python
import functools
import itertools
import math

import jax
import jax.numpy as jnp
from jax import lax
from jax.experimental import pallas as pl
from jax.experimental.pallas import tpu as pltpu
from jax.sharding import PartitionSpec as P

MESH = pl.DeviceIdType.MESH
HIST = 7
SWEEPS = 3
HALO = 3
SHIFT = 0.15
MIX = 0.7
DIAG = 6.0 + SHIFT
PAIRS = [(i, j) for i in range(HIST) for j in range(i + 1)]
ZR = 5
SLOT = 16


def sweep_weights():
    upper = (SHIFT + 12.0) / DIAG
    lower = upper / 3.0
    return [
        1.0
        / (
            (upper + lower) / 2.0
            + (upper - lower) / 2.0 * math.cos(math.pi * (2 * k - 1) / (2 * SWEEPS))
        )
        for k in range(1, SWEEPS + 1)
    ]


W1, W2, W3 = sweep_weights()
A2 = ((1.0 - W2) * W1 + W2) / DIAG
B2 = W2 * W1 / DIAG / DIAG
K1 = MIX * (1.0 - W3)
K2 = MIX * W3 / DIAG


def unrolled(count, step, body, init=None):
    def turn(q, carry):
        for j in range(step):
            carry = body(q * step + j, carry)
        return carry

    return lax.fori_loop(0, count // step, turn, init)


def lanes(shape):
    return lax.broadcasted_iota(jnp.int32, shape, len(shape) - 1)


def pulay(total):
    gram = {}
    for k, (i, j) in enumerate(PAIRS):
        gram[i, j] = jnp.broadcast_to(total[:, k : k + 1], (8, 128))
    low, inv, mid = {}, [], []
    for j in range(HIST):
        pivot = gram[j, j]
        for k in range(j):
            pivot = pivot - low[j, k] * low[j, k]
        inv.append(lax.rsqrt(pivot))
        for i in range(j + 1, HIST):
            value = gram[i, j]
            for k in range(j):
                value = value - low[i, k] * low[j, k]
            low[i, j] = value * inv[j]
        value = 1.0
        for k in range(j):
            value = value - low[j, k] * mid[k]
        mid.append(value * inv[j])
    solved = [None] * HIST
    for j in reversed(range(HIST)):
        value = mid[j]
        for k in range(j + 1, HIST):
            value = value - low[k, j] * solved[k]
        solved[j] = value * inv[j]
    scale = 1.0 / functools.reduce(jnp.add, solved)
    return [value * scale for value in solved]


def spread(packs):
    ring = next(pack.shape[0] for pack in packs if pack is not None)
    place = lanes((ring, 128)) % SLOT
    strips = []
    for zr in range(ZR):
        value = jnp.zeros((ring, 128), jnp.float32)
        for q, pack in enumerate(packs):
            if pack is not None:
                moved = pltpu.roll(pack, (HALO * (q - zr)) % 128, 1)
                value = jnp.where((place >= HALO * q) & (place < HALO * (q + 1)), moved, value)
        strips.append(value)
    return strips


def relaxed(start, closed=False):
    ring = start[0].shape[0]
    place = lanes((ring, 128)) % SLOT
    inside = (place >= HALO) & (place < 3 * HALO)

    def keep(v):
        return jnp.where(inside, v, 0.0) if closed else v

    def nb(v):
        out = []
        for zr in range(ZR):
            before = v[zr - 1] if zr else pltpu.roll(v[ZR - 1], SLOT, 1)
            after = v[zr + 1] if zr < ZR - 1 else pltpu.roll(v[0], 128 - SLOT, 1)
            total = before + after
            total = total + pltpu.roll(v[zr], 1, 0) + pltpu.roll(v[zr], ring - 1, 0)
            out.append(total + pltpu.roll(v[zr], 1, 1) + pltpu.roll(v[zr], 127, 1))
        return out

    r = [keep(6.0 * v - n) for v, n in zip(start, nb(start))]
    u = [keep(A2 * v + B2 * n) for v, n in zip(r, nb(r))]
    return [K1 * v + K2 * (s + n) for v, s, n in zip(u, r, nb(u))]


def exchange(sizes, dens, res, acc, from_left, from_right, strip, weights,
             R, D, C, T1, T2, G1, G2, packs, own_left, own_right,
             load_sem, dens_sem, bulk_send, bulk_recv,
             edge_send, edge_recv, gram_send, gram_recv, entered):
    NX, NY, NZ = sizes
    chips = NZ // 2
    nz, ny = res.shape[1], res.shape[2]
    ring = R.shape[2]
    gx, gy, gz = lax.axis_index("gx"), lax.axis_index("gy"), lax.axis_index("gz")

    def device(dx=0, dy=0, dz=0):
        return {
            "gx": lax.rem(gx + dx % NX, NX),
            "gy": lax.rem(gy + dy % NY, NY),
            "gz": lax.rem(gz + dz % NZ, NZ),
        }

    chip, core = gz // 2, lax.rem(gz, 2)

    def in_plane(dx, dy, other):
        to = device(dx=dx, dy=dy)
        if other:
            to["gz"] = 2 * chip + (1 - core)
        return to

    def along(step):
        to = lax.rem(chip + step, chips)
        return dict(device(), gz=2 * to + core), to > chip

    def hops(step):
        sizes_here = (NX, NY, 2) if len(step) == 3 else (chips,)
        return -sum(min(v, n - v) for v, n in zip(step, sizes_here))

    steps = sorted(itertools.product(range(NX), range(NY), range(2)), key=hops)
    plane_peers = [in_plane(*step) for step in steps if any(step)]
    line_peers = [along(*step) for step in sorted([(k,) for k in range(1, chips)], key=hops)]
    across = 2 * core - 1
    next_peers = [
        dict(device(dy=dy), gz=lax.rem(gz + across + NZ, NZ)) for dy in (-1, 0, 1)
    ]
    bottom, top = gz == 0, gz == NZ - 1
    barrier = pltpu.get_barrier_semaphore()

    def greet(semaphore, peer):
        pl.semaphore_signal(semaphore, inc=1, device_id=peer, device_id_type=MESH)

    def wait(semaphore, amount):
        pl.when(amount > 0)(functools.partial(pl.semaphore_wait, semaphore, amount))

    chunks = load_sem.shape[0]
    depth = nz // chunks
    loads = []
    for c in range(chunks):
        copy = pltpu.make_async_copy(
            res.at[:, pl.ds(c * depth, depth)],
            R.at[:, pl.ds(HALO + c * depth, depth), pl.ds(0, ny)],
            load_sem.at[c],
        )
        copy.start()
        loads.append(copy)
    dens_copy = pltpu.make_async_copy(dens, D, dens_sem)
    dens_copy.start()

    for peer, above in line_peers:
        pl.when(above)(functools.partial(greet, barrier, peer))
    for peer in plane_peers:
        greet(barrier, peer)

    @pl.when(jnp.logical_not(top))
    def _():
        for peer in next_peers:
            greet(barrier, peer)

    main = pl.ds(HALO, nz)
    inner = pl.ds(0, ny)
    end_z = HALO + nz
    moves = [
        (res.at[:, :, pl.ds(0, 3)], R.at[:, main, pl.ds(ny, 3)], device(dy=-1)),
        (res.at[:, :, pl.ds(ny - 3, 3)], R.at[:, main, pl.ds(ring - 3, 3)], device(dy=1)),
        (res.at[:, pl.ds(0, 3)], R.at[:, pl.ds(end_z, 3), inner], device(dz=-1)),
        (res.at[:, pl.ds(nz - 3, 3)], R.at[:, pl.ds(0, 3), inner], device(dz=1)),
    ]
    for sy, sz in itertools.product((-1, 1), (-1, 1)):
        zs, zd = (0, end_z) if sz < 0 else (nz - 2, 1)
        ys, yd = (0, ny) if sy < 0 else (ny - 2, ring - 2)
        moves.append((
            res.at[:, pl.ds(zs, 2), pl.ds(ys, 2)],
            R.at[:, pl.ds(zd, 2), pl.ds(yd, 2)],
            device(dy=sy, dz=sz),
        ))
    bulk = [
        pltpu.make_async_remote_copy(
            src, dst, bulk_send.at[k], bulk_recv.at[k], device_id=peer, device_id_type=MESH
        )
        for k, (src, dst, peer) in enumerate(moves)
    ]
    def plane_products(z, sums):
        sums = list(sums)
        for t in range(ny // 8):
            rows = [R[i, HALO + z, 8 * t : 8 * t + 8, :] for i in range(HIST)]
            for k, (i, j) in enumerate(PAIRS):
                sums[k] = sums[k] + rows[i] * rows[j]
        return tuple(sums)

    sums = tuple(jnp.zeros((8, 128), jnp.float32) for _ in PAIRS)
    for c in range(chunks):
        loads[c].wait()
        sums = lax.fori_loop(c * depth, (c + 1) * depth, plane_products, sums)
    lane = lanes((8, 128))
    partial = jnp.zeros((8, 128), jnp.float32)
    for k in range(len(PAIRS)):
        partial = jnp.where(lane == k, jnp.sum(sums[k], axis=1, keepdims=True), partial)
    row = jnp.sum(partial, axis=0, keepdims=True)

    def share(buf, slot, value, peers, phase):
        buf[slot] = value
        for peer in peers:
            pltpu.make_async_remote_copy(
                buf.at[slot], buf.at[slot], gram_send.at[phase], gram_recv.at[phase],
                device_id=peer, device_id_type=MESH,
            ).start()
        return buf.at[pl.ds(0, len(peers))]

    def summed(buf, others, phase):
        pltpu.make_async_copy(others, others, gram_recv.at[phase]).wait()
        total = buf[0]
        for k in range(1, buf.shape[0]):
            total = total + buf[k]
        return total

    few = len(next_peers)
    pl.semaphore_wait(barrier, len(plane_peers) + chip + few - few * bottom.astype(jnp.int32))
    others1 = share(G1, (gx * NY + gy) * 2 + core, row, plane_peers, 0)
    for peer, above in line_peers:
        pl.when(jnp.logical_not(above))(functools.partial(greet, entered.at[1], peer))

    @pl.when(top)
    def _():
        for peer in next_peers:
            greet(entered.at[0], peer)

    over = [bottom if k in (2, 4, 6) else None for k in range(len(bulk))]
    for copy, late in zip(bulk, over):
        if late is None:
            copy.start()
        else:
            pl.when(jnp.logical_not(late))(copy.start)

    @pl.when(bottom)
    def _():
        pl.semaphore_wait(entered.at[0], few)
        for k in (2, 4, 6):
            bulk[k].start()

    plane_row = summed(G1, others1, 0)
    wait(entered.at[1], chips - 1 - chip)
    others2 = share(G2, chip, plane_row, [peer for peer, _ in line_peers], 1)

    def pack_rows(low, high, i, _):
        wide = lanes((high - low, 128))
        for v in range((ZR + 1) // 2):
            part = jnp.zeros((high - low, 128), jnp.float32)
            for zr in range(2 * v, min(2 * v + 2, ZR)):
                for p in range(zr, nz + 4, ZR):
                    base = (p // ZR) * SLOT + 2 * HALO * (zr - 2 * v)
                    here = (wide >= base) & (wide < base + 2 * HALO)
                    moved = pltpu.roll(R[i, p + 1, low:high], (base + HALO) % 128, 1)
                    part = jnp.where(here, moved, part)
            packs[i, v, low:high] = part

    for copy in bulk[2:4]:
        copy.wait_recv()
    lax.fori_loop(0, HIST, functools.partial(pack_rows, 0, ny), None)
    for copy in bulk[:2] + bulk[4:]:
        copy.wait_recv()
    for i in range(HIST):
        pack_rows(ny, ring, i, None)
    wide = lanes((ring, 128))

    total = summed(G2, others2, 1)
    shares = pulay(total)
    for i in range(HIST):
        weights[i] = shares[i]
    shares = [weights[i] for i in range(HIST)]
    tiles = ring // 8

    def weighted(entries):
        out = None
        for share_i, entry in zip(shares, entries):
            term = share_i[None] * entry.reshape(-1, 8, 128)
            out = term if out is None else out + term
        return out.reshape(-1, 128)

    parts = [weighted([packs[i, v] for i in range(HIST)]) for v in range((ZR + 1) // 2)]
    place = wide % SLOT
    for side, own in enumerate((own_right, own_left)):
        edge = jnp.zeros((ring, 128), jnp.float32)
        for zr in range(ZR):
            source = 2 * HALO * (zr % 2) + HALO * side
            moved = pltpu.roll(parts[zr // 2], (HALO * zr - source) % 128, 1)
            edge = jnp.where((place >= HALO * zr) & (place < HALO * (zr + 1)), moved, edge)
        own[...] = edge
    edges = [
        pltpu.make_async_remote_copy(
            own_left, from_right, edge_send.at[0], edge_recv.at[0],
            device_id=device(dx=-1), device_id_type=MESH,
        ),
        pltpu.make_async_remote_copy(
            own_right, from_left, edge_send.at[1], edge_recv.at[1],
            device_id=device(dx=1), device_id_type=MESH,
        ),
    ]
    for copy in edges:
        copy.start()

    def combine(k, _):
        C[k] = weighted([R[i, k] for i in range(HIST)])

    unrolled(nz + 2 * HALO, (nz + 2 * HALO) // 2, combine)

    first, last = wide == 0, wide == 127

    def around(v):
        total = pltpu.roll(v, 1, 0) + pltpu.roll(v, ring - 1, 0)
        total = total + jnp.where(first, 0.0, pltpu.roll(v, 1, 1))
        return total + jnp.where(last, 0.0, pltpu.roll(v, 127, 1))

    def sweep1(k, _):
        v = C[k + 1]
        T1[k] = 6.0 * v - (C[k] + C[k + 2] + around(v))

    def sweep2(k, _):
        v = T1[k + 1]
        T2[k] = A2 * v + B2 * (T1[k] + T1[k + 2] + around(v))

    def sweep3(k, _):
        v = T2[k + 1]
        out = K1 * v + K2 * (T1[k + 2] + T2[k] + T2[k + 2] + around(v))
        acc[k] = out[:ny] + weighted([D[i, k] for i in range(HIST)])

    unrolled(nz + 4, 18, sweep1)
    unrolled(nz + 2, (nz + 2) // 2, sweep2)
    dens_copy.wait()
    unrolled(nz, 16, sweep3)
    own = spread((None, own_left[...], own_right[...], None))
    for zr, (a, b) in enumerate(zip(relaxed(own), relaxed(own, True))):
        strip[zr] = (a - b)[:ny]

    for copy in edges:
        copy.wait()
    for copy in bulk:
        copy.wait_send()
    for phase, others in enumerate((others1, others2)):
        pltpu.make_async_copy(others, others, gram_send.at[phase]).wait()


def finish(acc, from_left, from_right, strip, weights, out, coeffs, buf, row_buf, sem, row_sem):
    nz, ny = acc.shape[0], acc.shape[1]
    coeff_lane = lanes((1, 128))
    row = jnp.zeros((1, 128), jnp.float32)
    for i in range(HIST):
        row = jnp.where(coeff_lane == i, weights[i, 0:1, :], row)
    row_buf[...] = row[:, :HIST]
    row_copy = pltpu.make_async_copy(row_buf, coeffs, row_sem)
    row_copy.start()

    outer = spread((from_left[...], None, None, from_right[...]))
    change = [v[:ny] + strip[zr] for zr, v in enumerate(relaxed(outer))]
    lane = lanes((ny, 128))
    near, far = lane < HALO, lane >= 128 - HALO
    chunks = sem.shape[0]
    copies = []
    for z in range(nz):
        zq, zr = divmod(z + 2, ZR)
        at_left = pltpu.roll(change[zr], (-(SLOT * zq + HALO)) % 128, 1)
        at_right = pltpu.roll(change[zr], (125 - (SLOT * zq + 2 * HALO)) % 128, 1)
        buf[z] = acc[z] + jnp.where(near, at_left, jnp.where(far, at_right, 0.0))
        depth = nz // chunks
        if z % depth == depth - 1:
            c = z // depth
            part = pl.ds(c * depth, depth)
            copy = pltpu.make_async_copy(buf.at[part], out.at[part], sem.at[c])
            copy.start()
            copies.append(copy)
    for copy in copies:
        copy.wait()
    row_copy.wait()


def on_device(sizes, densities, residuals):
    _, nz, ny, nx = residuals.shape
    ring, deep = ny + 8, nz + 2 * HALO
    f32 = jnp.float32
    vmem, hbm = pl.BlockSpec(memory_space=pltpu.VMEM), pl.BlockSpec(memory_space=pltpu.HBM)
    edge = pltpu.VMEM((ring, nx), f32)
    NX, NY, NZ = sizes
    dma = pltpu.SemaphoreType.DMA
    middle = pl.pallas_call(
        functools.partial(exchange, sizes),
        out_shape=(
            pltpu.VMEM((nz, ny, nx), f32), edge, edge,
            pltpu.VMEM((ZR, ny, nx), f32), pltpu.VMEM((HIST, 8, 128), f32),
        ),
        in_specs=[hbm, hbm],
        out_specs=(vmem,) * 5,
        scratch_shapes=[
            pltpu.VMEM((HIST, deep, ring, nx), f32),
            pltpu.VMEM((HIST, nz, ny, nx), f32),
            pltpu.VMEM((deep, ring, nx), f32),
            pltpu.VMEM((deep - 2, ring, nx), f32),
            pltpu.VMEM((deep - 4, ring, nx), f32),
            pltpu.VMEM((NX * NY * 2, 1, 128), f32),
            pltpu.VMEM((NZ // 2, 1, 128), f32),
            pltpu.VMEM((HIST, (ZR + 1) // 2, ring, nx), f32),
            edge, edge,
            dma((8,)), dma(()), dma((8,)), dma((8,)), dma((2,)), dma((2,)), dma((2,)), dma((2,)),
            pltpu.SemaphoreType.REGULAR((2,)),
        ],
        compiler_params=pltpu.CompilerParams(
            collective_id=0, has_side_effects=True, vmem_limit_bytes=60 << 20
        ),
    )(densities, residuals)
    density, coeffs = pl.pallas_call(
        finish,
        out_shape=(
            jax.ShapeDtypeStruct((nz, ny, nx), f32),
            jax.ShapeDtypeStruct((1, HIST), f32),
        ),
        in_specs=[vmem] * 5,
        out_specs=(hbm, hbm),
        scratch_shapes=[
            pltpu.VMEM((nz, ny, nx), f32), pltpu.VMEM((1, HIST), f32), dma((4,)), dma(()),
        ],
        compiler_params=pltpu.CompilerParams(vmem_limit_bytes=16 << 20),
    )(*middle)
    return density, coeffs.reshape(HIST)


def solution(mesh):
    sizes = tuple(mesh.shape[a] for a in ("gx", "gy", "gz"))
    spec = P(None, "gz", "gy", "gx")
    return jax.shard_map(
        functools.partial(on_device, sizes),
        mesh=mesh,
        in_specs=(spec, spec),
        out_specs=(P("gz", "gy", "gx"), P()),
        check_vma=False,
    )
```

time: 35.4 us -> 24.7 us (0.70)
  Pallas kernels: 34.7 us -> 24 us
    pallas_call x1, Pallas kernels: 32.4 us -> 22.6 us  [on_device(): pl.pallas_call(functools.partial(exchange, sizes), out_shape=(pltpu.VMEM(...]
    pallas_call x1, Pallas kernels: 2.35 us -> 1.42 us  [on_device(): pl.pallas_call(finish, out_shape=(jax.ShapeDtypeStruct((nz, ny, nx), f32)...]
where the time goes in v2:
time: 24.7 us; the launch traced here: 24.6 us
  Pallas kernels  24 us (97%)
  between operations  0.64 us (3%)
    pallas_call x1, Pallas kernels, on_device(): pl.pallas_call(functools.partial(exchange, sizes), out_shape=(pltpu.VMEM(...  22.6 us
    pallas_call x1, Pallas kernels, on_device(): pl.pallas_call(finish, out_shape=(jax.ShapeDtypeStruct((nz, ny, nx), f32)...  1.42 us

profile of v2, /device:TPU:1, one launch (start us, length us, event | category | flops | bytes accessed | tf_op | source)
XLA Modules:
  0.0 24.6 jit_solution(15607224793504034792)
XLA Ops:
  0.6 22.6 %shard_map.41 = (f32[32,32,128]{2,1,0:T(8,128)S(1)}, f32[40,128]{1,0:T(8,128)S(1)}, f32[40,128]{1,0:T(8,128)S(1)}, f32[5,32,128]{2,1,0:T(8,128)S(1)}, f32[7,8,128]{2,1,0:T(8,128)S(1)}) custom-call(f32[7,32,32,128]{3,2,1,0:T(8,128)} %dens.1, f32[7,32,32,128]{3,2,1,0:T(8,128)} %res.1), custom_call_target="tpu_custom_call" | custom-call | tf_op jit(solution)/shard_map/pallas_call | solution.py:420
  23.2 1.4 %shard_map.42 = (f32[32,32,128]{2,1,0:T(8,128)}, f32[1,7]{1,0:T(1,128)}) custom-call(f32[32,32,128]{2,1,0:T(8,128)S(1)} %get-tuple-element.9.acc, f32[40,128]{1,0:T(8,128)S(1)} %get-tuple-element.10.from_left, f32[40,128]{1,0:T(8,128)S(1)} %get-tuple-element.11.from_right, f32[5,32,128]{2,1,0:T(8,128)S(1)} %get-tuple-element.12.strip, ...), custom_call_target="tpu_custom_call" | custom-call | tf_op jit(solution)/shard_map/pallas_call | solution.py:445

commit v3 on v2

--- a/solution.py
+++ b/solution.py
@@ -83,27 +83,21 @@
     return [value * scale for value in solved]
 
 
-def spread(packs):
-    ring = next(pack.shape[0] for pack in packs if pack is not None)
+def spread(left, right):
+    ring = left.shape[0]
     place = lanes((ring, 128)) % SLOT
     strips = []
     for zr in range(ZR):
         value = jnp.zeros((ring, 128), jnp.float32)
-        for q, pack in enumerate(packs):
-            if pack is not None:
-                moved = pltpu.roll(pack, (HALO * (q - zr)) % 128, 1)
-                value = jnp.where((place >= HALO * q) & (place < HALO * (q + 1)), moved, value)
+        for q, pack in ((0, left), (3, right)):
+            moved = pltpu.roll(pack, (HALO * (q - zr)) % 128, 1)
+            value = jnp.where((place >= HALO * q) & (place < HALO * (q + 1)), moved, value)
         strips.append(value)
     return strips
 
 
-def relaxed(start, closed=False):
+def relaxed(start):
     ring = start[0].shape[0]
-    place = lanes((ring, 128)) % SLOT
-    inside = (place >= HALO) & (place < 3 * HALO)
-
-    def keep(v):
-        return jnp.where(inside, v, 0.0) if closed else v
 
     def nb(v):
         out = []
@@ -115,13 +109,13 @@
             out.append(total + pltpu.roll(v[zr], 1, 1) + pltpu.roll(v[zr], 127, 1))
         return out
 
-    r = [keep(6.0 * v - n) for v, n in zip(start, nb(start))]
-    u = [keep(A2 * v + B2 * n) for v, n in zip(r, nb(r))]
+    r = [6.0 * v - n for v, n in zip(start, nb(start))]
+    u = [A2 * v + B2 * n for v, n in zip(r, nb(r))]
     return [K1 * v + K2 * (s + n) for v, s, n in zip(u, r, nb(u))]
 
 
-def exchange(sizes, dens, res, acc, from_left, from_right, strip, weights,
-             R, D, C, T1, T2, G1, G2, packs, own_left, own_right,
+def exchange(sizes, dens, res, acc, from_left, from_right, own_left, own_right, weights,
+             R, D, C, T1, T2, G1, G2, packs,
              load_sem, dens_sem, bulk_send, bulk_recv,
              edge_send, edge_recv, gram_send, gram_recv, entered):
     NX, NY, NZ = sizes
@@ -212,7 +206,8 @@
         ))
     bulk = [
         pltpu.make_async_remote_copy(
-            src, dst, bulk_send.at[k], bulk_recv.at[k], device_id=peer, device_id_type=MESH
+            src, dst, bulk_send, bulk_recv.at[0 if k in (2, 3) else 1],
+            device_id=peer, device_id_type=MESH,
         )
         for k, (src, dst, peer) in enumerate(moves)
     ]
@@ -277,6 +272,11 @@
     plane_row = summed(G1, others1, 0)
     wait(entered.at[1], chips - 1 - chip)
     others2 = share(G2, chip, plane_row, [peer for peer, _ in line_peers], 1)
+
+    def arrived(semaphore, rows):
+        width = ring if rows % ring == 0 else 8
+        view = R.at[:, pl.ds(0, rows // width), pl.ds(0, width)]
+        pltpu.make_async_copy(view, view, semaphore).wait()
 
     def pack_rows(low, high, i, _):
         wide = lanes((high - low, 128))
@@ -290,14 +290,14 @@
                     part = jnp.where(here, moved, part)
             packs[i, v, low:high] = part
 
-    for copy in bulk[2:4]:
-        copy.wait_recv()
+    arrived(bulk_recv.at[0], 2 * HALO * ny)
     lax.fori_loop(0, HIST, functools.partial(pack_rows, 0, ny), None)
-    for copy in bulk[:2] + bulk[4:]:
-        copy.wait_recv()
+    arrived(bulk_recv.at[1], 2 * HALO * nz + 16)
     for i in range(HIST):
         pack_rows(ny, ring, i, None)
     wide = lanes((ring, 128))
+    arrived(bulk_send, 2 * HALO * (nz + ny) + 16)
+    pltpu.make_async_copy(others1, others1, gram_send.at[0]).wait()
 
     total = summed(G2, others2, 1)
     shares = pulay(total)
@@ -322,30 +322,20 @@
             moved = pltpu.roll(parts[zr // 2], (HALO * zr - source) % 128, 1)
             edge = jnp.where((place >= HALO * zr) & (place < HALO * (zr + 1)), moved, edge)
         own[...] = edge
-    edges = [
+    for own, there, dx in ((own_left, from_right, -1), (own_right, from_left, 1)):
         pltpu.make_async_remote_copy(
-            own_left, from_right, edge_send.at[0], edge_recv.at[0],
-            device_id=device(dx=-1), device_id_type=MESH,
-        ),
-        pltpu.make_async_remote_copy(
-            own_right, from_left, edge_send.at[1], edge_recv.at[1],
-            device_id=device(dx=1), device_id_type=MESH,
-        ),
-    ]
-    for copy in edges:
-        copy.start()
+            own, there, edge_send, edge_recv, device_id=device(dx=dx), device_id_type=MESH
+        ).start()
 
     def combine(k, _):
         C[k] = weighted([R[i, k] for i in range(HIST)])
 
     unrolled(nz + 2 * HALO, (nz + 2 * HALO) // 2, combine)
 
-    first, last = wide == 0, wide == 127
-
-    def around(v):
-        total = pltpu.roll(v, 1, 0) + pltpu.roll(v, ring - 1, 0)
-        total = total + jnp.where(first, 0.0, pltpu.roll(v, 1, 1))
-        return total + jnp.where(last, 0.0, pltpu.roll(v, 127, 1))
+    def around(v, rows=ring):
+        total = (pltpu.roll(v, 1, 0) + pltpu.roll(v, ring - 1, 0))[:rows]
+        v = v[:rows]
+        return total + pltpu.roll(v, 1, 1) + pltpu.roll(v, 127, 1)
 
     def sweep1(k, _):
         v = C[k + 1]
@@ -357,26 +347,22 @@
 
     def sweep3(k, _):
         v = T2[k + 1]
-        out = K1 * v + K2 * (T1[k + 2] + T2[k] + T2[k + 2] + around(v))
-        acc[k] = out[:ny] + weighted([D[i, k] for i in range(HIST)])
+        near_z = T1[k + 2, :ny] + T2[k, :ny] + T2[k + 2, :ny]
+        out = K1 * v[:ny] + K2 * (near_z + around(v, ny))
+        acc[k] = out + weighted([D[i, k] for i in range(HIST)])
 
     unrolled(nz + 4, 18, sweep1)
     unrolled(nz + 2, (nz + 2) // 2, sweep2)
     dens_copy.wait()
     unrolled(nz, 16, sweep3)
-    own = spread((None, own_left[...], own_right[...], None))
-    for zr, (a, b) in enumerate(zip(relaxed(own), relaxed(own, True))):
-        strip[zr] = (a - b)[:ny]
-
-    for copy in edges:
-        copy.wait()
-    for copy in bulk:
-        copy.wait_send()
-    for phase, others in enumerate((others1, others2)):
-        pltpu.make_async_copy(others, others, gram_send.at[phase]).wait()
-
-
-def finish(acc, from_left, from_right, strip, weights, out, coeffs, buf, row_buf, sem, row_sem):
+    both = C.at[pl.ds(0, 2)]
+    pltpu.make_async_copy(both, both, edge_recv).wait()
+    pltpu.make_async_copy(both, both, edge_send).wait()
+    pltpu.make_async_copy(others2, others2, gram_send.at[1]).wait()
+
+
+def finish(acc, from_left, from_right, own_left, own_right, weights, out, coeffs,
+           buf, row_buf, sem, row_sem):
     nz, ny = acc.shape[0], acc.shape[1]
     coeff_lane = lanes((1, 128))
     row = jnp.zeros((1, 128), jnp.float32)
@@ -386,8 +372,8 @@
     row_copy = pltpu.make_async_copy(row_buf, coeffs, row_sem)
     row_copy.start()
 
-    outer = spread((from_left[...], None, None, from_right[...]))
-    change = [v[:ny] + strip[zr] for zr, v in enumerate(relaxed(outer))]
+    beyond = spread(from_left[...] - own_right[...], from_right[...] - own_left[...])
+    change = [v[:ny] for v in relaxed(beyond)]
     lane = lanes((ny, 128))
     near, far = lane < HALO, lane >= 128 - HALO
     chunks = sem.shape[0]
@@ -420,11 +406,11 @@
     middle = pl.pallas_call(
         functools.partial(exchange, sizes),
         out_shape=(
-            pltpu.VMEM((nz, ny, nx), f32), edge, edge,
-            pltpu.VMEM((ZR, ny, nx), f32), pltpu.VMEM((HIST, 8, 128), f32),
+            pltpu.VMEM((nz, ny, nx), f32), edge, edge, edge, edge,
+            pltpu.VMEM((HIST, 8, 128), f32),
         ),
         in_specs=[hbm, hbm],
-        out_specs=(vmem,) * 5,
+        out_specs=(vmem,) * 6,
         scratch_shapes=[
             pltpu.VMEM((HIST, deep, ring, nx), f32),
             pltpu.VMEM((HIST, nz, ny, nx), f32),
@@ -434,8 +420,7 @@
             pltpu.VMEM((NX * NY * 2, 1, 128), f32),
             pltpu.VMEM((NZ // 2, 1, 128), f32),
             pltpu.VMEM((HIST, (ZR + 1) // 2, ring, nx), f32),
-            edge, edge,
-            dma((8,)), dma(()), dma((8,)), dma((8,)), dma((2,)), dma((2,)), dma((2,)), dma((2,)),
+            dma((8,)), dma(()), dma(()), dma((2,)), dma(()), dma(()), dma((2,)), dma((2,)),
             pltpu.SemaphoreType.REGULAR((2,)),
         ],
         compiler_params=pltpu.CompilerParams(
@@ -448,7 +433,7 @@
             jax.ShapeDtypeStruct((nz, ny, nx), f32),
             jax.ShapeDtypeStruct((1, HIST), f32),
         ),
-        in_specs=[vmem] * 5,
+        in_specs=[vmem] * 6,
         out_specs=(hbm, hbm),
         scratch_shapes=[
             pltpu.VMEM((nz, ny, nx), f32), pltpu.VMEM((1, HIST), f32), dma((4,)), dma(()),

time: 24.7 us -> 24 us (0.972)
  Pallas kernels: 24 us -> 23.3 us
    pallas_call x1, Pallas kernels: 22.6 us -> 21.8 us  [on_device(): pl.pallas_call(functools.partial(exchange, sizes), out_shape=(pltpu.VMEM(...]
where the time goes in v3:
time: 24 us; the launch traced here: 23.9 us
  Pallas kernels  23.3 us (97%)
  between operations  0.64 us (3%)
    pallas_call x1, Pallas kernels, on_device(): pl.pallas_call(functools.partial(exchange, sizes), out_shape=(pltpu.VMEM(...  21.8 us
    pallas_call x1, Pallas kernels, on_device(): pl.pallas_call(finish, out_shape=(jax.ShapeDtypeStruct((nz, ny, nx), f32)...  1.42 us

profile of v3, /device:TPU:1, one launch (start us, length us, event | category | flops | bytes accessed | tf_op | source)
XLA Modules:
  0.0 23.9 jit_solution(4719020183044238612)
XLA Ops:
  0.6 21.8 %shard_map.41 = (f32[32,32,128]{2,1,0:T(8,128)S(1)}, f32[40,128]{1,0:T(8,128)S(1)}, f32[40,128]{1,0:T(8,128)S(1)}, f32[40,128]{1,0:T(8,128)S(1)}, f32[40,128]{1,0:T(8,128)S(1)}, /*index=5*/f32[7,8,128]{2,1,0:T(8,128)S(1)}) custom-call(f32[7,32,32,128]{3,2,1,0:T(8,128)} %dens.1, f32[7,32,32,128]{3,2,1,0:T(8,128)} %res.1), custom_call_target="tpu_custom_call" | custom-call | tf_op jit(solution)/shard_map/pallas_call | solution.py:406
  22.5 1.4 %shard_map.42 = (f32[32,32,128]{2,1,0:T(8,128)}, f32[1,7]{1,0:T(1,128)}) custom-call(f32[32,32,128]{2,1,0:T(8,128)S(1)} %get-tuple-element.10.acc, f32[40,128]{1,0:T(8,128)S(1)} %get-tuple-element.11.from_left, f32[40,128]{1,0:T(8,128)S(1)} %get-tuple-element.12.from_right, f32[40,128]{1,0:T(8,128)S(1)} %get-tuple-element.13.own_left, ...), custom_call_target="tpu_custom_call" | custom-call | tf_op jit(solution)/shard_map/pallas_call | solution.py:430
